TPU v7x, 32 devices: a whole 2x2x4 slice. The times are simulated.
32 devices in a mesh: xy: 16 (over z, y, core), gz: 2 (over x).
Axes of the slice: x: 2, y: 2, z: 4, core: 2. Of those that a mesh axis runs over, the one named last changes fastest.
Arguments:
- e_check: float32 [3, 128, 4, 1024], P(None, 'xy', 'gz'), may hold values from -6 to 6
- h_check: float32 [3, 128, 4, 1024], P(None, 'xy', 'gz'), may hold values from -6 to 6
- adj_e: float32 [3, 128, 4, 1024], P(None, 'xy', 'gz'), may hold values from -6 to 6
- adj_h: float32 [3, 128, 4, 1024], P(None, 'xy', 'gz'), may hold values from -6 to 6
- material: int32 [128, 4, 1024], P('xy', 'gz'), may hold values from 0 to 3
- owner: int32 [128, 4, 1024], P('xy', 'gz'), may hold values from 0 to 7
- permittivity: float32 [4], replicated, may hold values from 1 to 4
Outputs:
- adj_e_out: float32 [3, 128, 4, 1024], P(None, 'xy', 'gz')
- adj_h_out: float32 [3, 128, 4, 1024], P(None, 'xy', 'gz')
- height_grad: float32 [8], replicated
All inputs are finite; a program needn't handle non-finite values.
Results may differ from a plain program's by a relative error of at most 0.0003.
Values sent between devices are 32-bit elements; how exact they have to be, the bound alone decides.
A program may use at most 64 MiB of HBM per device.

v0:
```python
import jax
import jax.numpy as jnp
from jax import lax
from jax.sharding import PartitionSpec as P

NI = 8


COURANT = 0.5


def shifted(value, axis, steps):
    count = lax.axis_size(axis)
    leading, last = (max(0, -steps), min(count, count - steps))
    return lax.ppermute(value, axis, [(source, source + steps) for source in range(leading, last)])


def ahead_diff(values, edge_plane, dim_axis):
    dim_axis = values.ndim + dim_axis
    count = values.shape[dim_axis]
    later = jnp.concatenate(
        [lax.slice_in_dim(values, 1, count, axis=dim_axis), edge_plane], axis=dim_axis
    )
    return later - values


def behind_diff(values, edge_plane, dim_axis):
    dim_axis = values.ndim + dim_axis
    count = values.shape[dim_axis]
    earlier = jnp.concatenate(
        [edge_plane, lax.slice_in_dim(values, 0, count - 1, axis=dim_axis)], axis=dim_axis
    )
    return values - earlier


def curl_fwd(fields):
    above_x = shifted(fields[..., 1:3, :1, :, :], "xy", -1)
    above_z = shifted(fields[..., 0:2, :, :1, :], "gz", -1)
    comp_x = fields[..., 0, :, :, :]
    comp_y = fields[..., 1, :, :, :]
    comp_z = fields[..., 2, :, :, :]
    zero_y = jnp.zeros_like(comp_x[..., :1])
    curl_x = ahead_diff(comp_z, zero_y, -1) - ahead_diff(comp_y, above_z[..., 1, :, :, :], -2)
    curl_y = ahead_diff(comp_x, above_z[..., 0, :, :, :], -2) - ahead_diff(
        comp_z, above_x[..., 1, :, :, :], -3
    )
    curl_z = ahead_diff(comp_y, above_x[..., 0, :, :, :], -3) - ahead_diff(comp_x, zero_y, -1)
    return jnp.stack([curl_x, curl_y, curl_z], axis=-4)


def curl_bwd(fields):
    below_x = shifted(fields[..., 1:3, -1:, :, :], "xy", 1)
    below_z = shifted(fields[..., 0:2, :, -1:, :], "gz", 1)
    comp_x = fields[..., 0, :, :, :]
    comp_y = fields[..., 1, :, :, :]
    comp_z = fields[..., 2, :, :, :]
    zero_y = jnp.zeros_like(comp_x[..., :1])
    curl_x = behind_diff(comp_z, zero_y, -1) - behind_diff(comp_y, below_z[..., 1, :, :, :], -2)
    curl_y = behind_diff(comp_x, below_z[..., 0, :, :, :], -2) - behind_diff(
        comp_z, below_x[..., 1, :, :, :], -3
    )
    curl_z = behind_diff(comp_y, below_x[..., 0, :, :, :], -3) - behind_diff(comp_x, zero_y, -1)
    return jnp.stack([curl_x, curl_y, curl_z], axis=-4)


def interface_sums(weight, owner):
    onehot = (owner.reshape(-1, 1) == jnp.arange(NI, dtype=jnp.int32)[None, :]).astype(jnp.float32)
    return jnp.dot(weight.reshape(1, -1), onehot, precision=lax.Precision.HIGHEST)[0]


def body(e_check, h_check, adj_e, adj_h, material, owner, permittivity):
    e_coef = jnp.zeros(material.shape, jnp.float32)
    for kind_index in range(4):
        e_coef = e_coef + jnp.where(material == kind_index, COURANT / permittivity[kind_index], 0.0)
    electric = [e_check]
    magnetic = h_check
    adjoint_e = [adj_e]
    adjoint_h = adj_h
    for index_step in range(2):
        first = curl_fwd(jnp.stack([electric[-1], e_coef * adjoint_e[-1]], axis=0))
        magnetic = magnetic - COURANT * first[0]
        adjoint_h = adjoint_h + first[1]
        second = curl_bwd(jnp.stack([magnetic, adjoint_h], axis=0))
        electric.append(electric[-1] + e_coef * second[0])
        adjoint_e.append(adjoint_e[-1] - COURANT * second[1])
    partials = []
    for later_step in (2, 1):
        adjoint_now = adjoint_e[2 - later_step]
        weight = e_coef * jnp.sum(
            adjoint_now * (electric[later_step] - electric[later_step - 1]), axis=0
        )
        partials.append(interface_sums(weight, owner))
    gradient = jnp.zeros((NI,), jnp.float32)
    for partial_sum in partials:
        gradient = gradient + lax.psum(partial_sum, ("xy", "gz"))
    total_cells = (
        e_check.shape[1]
        * lax.axis_size("xy")
        * e_check.shape[2]
        * lax.axis_size("gz")
        * e_check.shape[3]
    )
    gradient = gradient / jnp.sqrt(jnp.float32(total_cells / NI))
    return (adjoint_e[-1], adjoint_h, gradient)


def solution(mesh):
    in_specs = (
        P(None, "xy", "gz", None),
        P(None, "xy", "gz", None),
        P(None, "xy", "gz", None),
        P(None, "xy", "gz", None),
        P("xy", "gz", None),
        P("xy", "gz", None),
        P(),
    )
    out_specs = (P(None, "xy", "gz", None), P(None, "xy", "gz", None), P())
    return jax.shard_map(body, mesh=mesh, in_specs=in_specs, out_specs=out_specs, check_vma=False)
```

profile of v0, /device:TPU:0, one launch (start us, length us, event | category | flops | bytes accessed | tf_op | source)
XLA Modules:
  0.0 94.5 jit_solution(2461075382136776131)
XLA Ops:
  0.6 1.4 %fusion.70 = (f32[1]{0:T(128)}, f32[1]{0:T(128)}, f32[1]{0:T(128)}, f32[1]{0:T(128)}) fusion(f32[4]{0:T(128)} %param.13), kind=kLoop, calls=%fused_computation.166 | loop fusion | bytes 32 | tf_op jit(solution)/shard_map/slice | solution.py:74
  4.8 0.9 fusion.65
  5.7 1.0 %multiply_bitcast_fusion.1 = f32[1,3,8,2,1024]{4,3,2,1,0:T(2,128)S(1)} fusion(f32[3,8,2,1024]{3,2,1,0:T(2,128)} %param.9, f32[8,2,1024]{2,1,0:T(2,128)S(1)} %fusion.65), kind=kLoop, calls=%fused_computation.68 | loop fusion | flops 49152 | bytes 458752 | tf_op jit(solution)/shard_map/stack | solution.py:80
  6.9 1.3 %collective-permute-start = (f32[2,2,8,1,1024]{4,3,2,1,0:T(1,128)S(1)}, f32[2,2,8,1,1024]{4,3,2,1,0:T(1,128)S(1)}, u32[]{:S(2)}, u32[]{:S(2)}) collective-permute-start(f32[2,2,8,1,1024]{4,3,2,1,0:T(1,128)S(1)} %fusion.22), channel_id=1, source_target_pairs={{1,0},{3,2},{5,4},{7,6},{9,8},{11,10},{13,12},{15,14},{17,16},{19,... | collective-permute-start | bytes 393224 | tf_op jit(solution)/shard_map/ppermute | solution.py:15
  8.2 1.3 %collective-permute-start.1 = (f32[2,2,1,2,1024]{4,3,2,1,0:T(2,128)S(1)}, f32[2,2,1,2,1024]{4,3,2,1,0:T(2,128)S(1)}, u32[]{:S(2)}, u32[]{:S(2)}) collective-permute-start(f32[2,2,1,2,1024]{4,3,2,1,0:T(2,128)S(1)} %pad_maximum_fusion.7), channel_id=1, source_target_pairs={{2,0},{4,2},{6,4},{8,6},{10,8},{12,10},{14,12},{16,14},{18,16},{20... | collective-permute-start | bytes 98312 | tf_op jit(solution)/shard_map/ppermute | solution.py:15
  9.5 0.2 fusion.33
  9.8 0.2 slice.290
  10.0 0.2 slice.305
  10.3 0.8 copy-done.6
  11.2 0.2 collective-permute-done.1
  11.3 3.4 %collective-permute-done = f32[2,2,8,1,1024]{4,3,2,1,0:T(1,128)S(1)} collective-permute-done((f32[2,2,8,1,1024]{4,3,2,1,0:T(1,128)S(1)}, f32[2,2,8,1,1024]{4,3,2,1,0:T(1,128)S(1)}, u32[]{:S(2)}, u32[]{:S(2)}) %collective-permute-start) | collective-permute-done | bytes 131104 | tf_op jit(solution)/shard_map/ppermute | solution.py:15
  14.7 0.2 fusion.37
  14.9 0.3 fusion.36
  15.3 0.2 pad_maximum_fusion
  15.5 0.7 copy-done.3
  16.3 0.2 fusion.67
  16.5 0.2 fusion.30
  16.7 2.1 %collective-permute-start.3 = (f32[2,2,1,2,1024]{4,3,2,1,0:T(2,128)S(1)}, f32[2,2,1,2,1024]{4,3,2,1,0:T(2,128)S(1)}, u32[]{:S(2)}, u32[]{:S(2)}) collective-permute-start(f32[2,2,1,2,1024]{4,3,2,1,0:T(2,128)S(1)} %pad_maximum_fusion.6), channel_id=1, source_target_pairs={{0,2},{2,4},{4,6},{6,8},{8,10},{10,12},{12,14},{14,16},{16,18},{18... | collective-permute-start | bytes 98312 | tf_op jit(solution)/shard_map/ppermute | solution.py:15
  18.9 0.2 fusion.21
  19.1 4.6 %collective-permute-start.2 = (f32[2,2,8,1,1024]{4,3,2,1,0:T(1,128)S(1)}, f32[2,2,8,1,1024]{4,3,2,1,0:T(1,128)S(1)}, u32[]{:S(2)}, u32[]{:S(2)}) collective-permute-start(f32[2,2,8,1,1024]{4,3,2,1,0:T(1,128)S(1)} %fusion.21), channel_id=1, source_target_pairs={{0,1},{2,3},{4,5},{6,7},{8,9},{10,11},{12,13},{14,15},{16,17},{18,... | collective-permute-start | bytes 393224 | tf_op jit(solution)/shard_map/ppermute | solution.py:15
  23.7 3.0 %collective-permute-done.2 = f32[2,2,8,1,1024]{4,3,2,1,0:T(1,128)S(1)} collective-permute-done((f32[2,2,8,1,1024]{4,3,2,1,0:T(1,128)S(1)}, f32[2,2,8,1,1024]{4,3,2,1,0:T(1,128)S(1)}, u32[]{:S(2)}, u32[]{:S(2)}) %collective-permute-start.2) | collective-permute-done | bytes 131104 | tf_op jit(solution)/shard_map/ppermute | solution.py:15
  26.7 0.2 fusion.43
  26.9 0.5 fusion.42
  27.4 0.2 pad_maximum_fusion.1
  27.6 0.7 copy-done.2
  28.3 0.3 fusion.68
  28.6 0.2 fusion.27
  28.8 1.3 %collective-permute-start.5 = (f32[2,2,1,2,1024]{4,3,2,1,0:T(2,128)S(1)}, f32[2,2,1,2,1024]{4,3,2,1,0:T(2,128)S(1)}, u32[]{:S(2)}, u32[]{:S(2)}) collective-permute-start(f32[2,2,1,2,1024]{4,3,2,1,0:T(2,128)S(1)} %pad_maximum_fusion.5), channel_id=1, source_target_pairs={{2,0},{4,2},{6,4},{8,6},{10,8},{12,10},{14,12},{16,14},{18,16},{20... | collective-permute-start | bytes 98312 | tf_op jit(solution)/shard_map/ppermute | solution.py:15
  30.4 0.2 slice.330
  30.6 0.2 slice.345
  30.9 1.3 %collective-permute-start.4 = (f32[2,2,8,1,1024]{4,3,2,1,0:T(1,128)S(1)}, f32[2,2,8,1,1024]{4,3,2,1,0:T(1,128)S(1)}, u32[]{:S(2)}, u32[]{:S(2)}) collective-permute-start(f32[2,2,8,1,1024]{4,3,2,1,0:T(1,128)S(1)} %fusion.20), channel_id=1, source_target_pairs={{1,0},{3,2},{5,4},{7,6},{9,8},{11,10},{13,12},{15,14},{17,16},{19,... | collective-permute-start | bytes 393224 | tf_op jit(solution)/shard_map/ppermute | solution.py:15
  32.2 6.7 %collective-permute-done.4 = f32[2,2,8,1,1024]{4,3,2,1,0:T(1,128)S(1)} collective-permute-done((f32[2,2,8,1,1024]{4,3,2,1,0:T(1,128)S(1)}, f32[2,2,8,1,1024]{4,3,2,1,0:T(1,128)S(1)}, u32[]{:S(2)}, u32[]{:S(2)}) %collective-permute-start.4) | collective-permute-done | bytes 131104 | tf_op jit(solution)/shard_map/ppermute | solution.py:15
  38.9 0.2 fusion.49
  39.1 0.3 fusion.48
  39.4 0.2 pad_maximum_fusion.2
  39.6 0.3 fusion.10
  39.9 0.2 fusion.24
  40.2 2.0 %collective-permute-start.7 = (f32[2,2,1,2,1024]{4,3,2,1,0:T(2,128)S(1)}, f32[2,2,1,2,1024]{4,3,2,1,0:T(2,128)S(1)}, u32[]{:S(2)}, u32[]{:S(2)}) collective-permute-start(f32[2,2,1,2,1024]{4,3,2,1,0:T(2,128)S(1)} %pad_maximum_fusion.4), channel_id=1, source_target_pairs={{0,2},{2,4},{4,6},{6,8},{8,10},{10,12},{12,14},{14,16},{16,18},{18... | collective-permute-start | bytes 98312 | tf_op jit(solution)/shard_map/ppermute | solution.py:15
  42.5 1.7 %collective-permute-start.6 = (f32[2,2,8,1,1024]{4,3,2,1,0:T(1,128)S(1)}, f32[2,2,8,1,1024]{4,3,2,1,0:T(1,128)S(1)}, u32[]{:S(2)}, u32[]{:S(2)}) collective-permute-start(f32[2,2,8,1,1024]{4,3,2,1,0:T(1,128)S(1)} %fusion.19), channel_id=1, source_target_pairs={{0,1},{2,3},{4,5},{6,7},{8,9},{10,11},{12,13},{14,15},{16,17},{18,... | collective-permute-start | bytes 393224 | tf_op jit(solution)/shard_map/ppermute | solution.py:15
  44.3 2.5 %collective-permute-done.6 = f32[2,2,8,1,1024]{4,3,2,1,0:T(1,128)S(1)} collective-permute-done((f32[2,2,8,1,1024]{4,3,2,1,0:T(1,128)S(1)}, f32[2,2,8,1,1024]{4,3,2,1,0:T(1,128)S(1)}, u32[]{:S(2)}, u32[]{:S(2)}) %collective-permute-start.6) | collective-permute-done | bytes 131104 | tf_op jit(solution)/shard_map/ppermute | solution.py:15
  46.8 0.2 fusion.55
  47.0 0.5 fusion.54
  47.5 0.2 pad_maximum_fusion.3
  47.7 1.2 %fusion.18 = (f32[8,2,1024]{2,1,0:T(2,128)S(1)}, f32[8,2,1024]{2,1,0:T(2,128)S(1)}, f32[3,8,2,1024]{3,2,1,0:T(2,128)}) fusion(f32[3,8,2,1024]{3,2,1,0:T(2,128)S(1)} %copy-done.2, f32[2,3,8,2,1024]{4,3,2,1,0:T(2,128)S(1)} %pad_maximum_fusion.3, f32[8,2,1024]{2,1,0:T(2,128)S(1)} %fusion.65, f32[3,8,2,1024]{3,2,1,0:T(2,128)S(1)} %copy-done, ...), kind=kLoop, calls=%fused_computation.69 | loop fusion | flops 655360 | bytes 1572864 | tf_op jit(solution)/shard_map/reduce_sum | solution.py:89
  49.3 0.7 convolution_bitcast_fusion
  50.0 0.7 fusion
  50.7 43.3 %psum.16 = f32[8]{0:T(128)S(1)} all-reduce(f32[8]{0:T(128)S(1)} %fusion), channel_id=1, replica_groups=mesh['xy'=16,'gz'=2] {'xy','gz'}, use_global_device_ids=true, to_apply=%region_1.2 | all-reduce | flops 8 | bytes 64 | tf_op jit(solution)/shard_map/psum | solution.py:95
  94.0 0.5 broadcast_multiply_fusion
  (49 shorter events, 1.6 us)
Async XLA Ops:
  5.7 1.1 %copy-start = (f32[3,8,2,1024]{3,2,1,0:T(2,128)S(1)}, f32[3,8,2,1024]{3,2,1,0:T(2,128)}, u32[]{:S(2)}) copy-start(f32[3,8,2,1024]{3,2,1,0:T(2,128)} %param.7) | copy-start | bytes 589828
  6.9 7.8 %collective-permute-start = (f32[2,2,8,1,1024]{4,3,2,1,0:T(1,128)S(1)}, f32[2,2,8,1,1024]{4,3,2,1,0:T(1,128)S(1)}, u32[]{:S(2)}, u32[]{:S(2)}) collective-permute-start(f32[2,2,8,1,1024]{4,3,2,1,0:T(1,128)S(1)} %fusion.22), channel_id=1, source_target_pairs={{1,0},{3,2},{5,4},{7,6},{9,8},{11,10},{13,12},{15,14},{17,16},{19,... | collective-permute-start | bytes 393224 | tf_op jit(solution)/shard_map/ppermute | solution.py:15
  8.2 3.1 %collective-permute-start.1 = (f32[2,2,1,2,1024]{4,3,2,1,0:T(2,128)S(1)}, f32[2,2,1,2,1024]{4,3,2,1,0:T(2,128)S(1)}, u32[]{:S(2)}, u32[]{:S(2)}) collective-permute-start(f32[2,2,1,2,1024]{4,3,2,1,0:T(2,128)S(1)} %pad_maximum_fusion.7), channel_id=1, source_target_pairs={{2,0},{4,2},{6,4},{8,6},{10,8},{12,10},{14,12},{16,14},{18,16},{20... | collective-permute-start | bytes 98312 | tf_op jit(solution)/shard_map/ppermute | solution.py:15
  10.3 0.8 copy-start.6
  15.3 0.9 copy-start.3
  15.3 1.0 %copy-start.4 = (f32[3,8,2,1024]{3,2,1,0:T(2,128)S(1)}, f32[3,8,2,1024]{3,2,1,0:T(2,128)}, u32[]{:S(2)}) copy-start(f32[3,8,2,1024]{3,2,1,0:T(2,128)} %param.10) | copy-start | bytes 589828
  16.7 7.0 %collective-permute-start.3 = (f32[2,2,1,2,1024]{4,3,2,1,0:T(2,128)S(1)}, f32[2,2,1,2,1024]{4,3,2,1,0:T(2,128)S(1)}, u32[]{:S(2)}, u32[]{:S(2)}) collective-permute-start(f32[2,2,1,2,1024]{4,3,2,1,0:T(2,128)S(1)} %pad_maximum_fusion.6), channel_id=1, source_target_pairs={{0,2},{2,4},{4,6},{6,8},{8,10},{10,12},{12,14},{14,16},{16,18},{18... | collective-permute-start | bytes 98312 | tf_op jit(solution)/shard_map/ppermute | solution.py:15
  19.1 7.5 %collective-permute-start.2 = (f32[2,2,8,1,1024]{4,3,2,1,0:T(1,128)S(1)}, f32[2,2,8,1,1024]{4,3,2,1,0:T(1,128)S(1)}, u32[]{:S(2)}, u32[]{:S(2)}) collective-permute-start(f32[2,2,8,1,1024]{4,3,2,1,0:T(1,128)S(1)} %fusion.21), channel_id=1, source_target_pairs={{0,1},{2,3},{4,5},{6,7},{8,9},{10,11},{12,13},{14,15},{16,17},{18,... | collective-permute-start | bytes 393224 | tf_op jit(solution)/shard_map/ppermute | solution.py:15
  27.4 0.9 copy-start.2
  28.8 3.3 %collective-permute-start.5 = (f32[2,2,1,2,1024]{4,3,2,1,0:T(2,128)S(1)}, f32[2,2,1,2,1024]{4,3,2,1,0:T(2,128)S(1)}, u32[]{:S(2)}, u32[]{:S(2)}) collective-permute-start(f32[2,2,1,2,1024]{4,3,2,1,0:T(2,128)S(1)} %pad_maximum_fusion.5), channel_id=1, source_target_pairs={{2,0},{4,2},{6,4},{8,6},{10,8},{12,10},{14,12},{16,14},{18,16},{20... | collective-permute-start | bytes 98312 | tf_op jit(solution)/shard_map/ppermute | solution.py:15
  30.9 8.0 %collective-permute-start.4 = (f32[2,2,8,1,1024]{4,3,2,1,0:T(1,128)S(1)}, f32[2,2,8,1,1024]{4,3,2,1,0:T(1,128)S(1)}, u32[]{:S(2)}, u32[]{:S(2)}) collective-permute-start(f32[2,2,8,1,1024]{4,3,2,1,0:T(1,128)S(1)} %fusion.20), channel_id=1, source_target_pairs={{1,0},{3,2},{5,4},{7,6},{9,8},{11,10},{13,12},{15,14},{17,16},{19,... | collective-permute-start | bytes 393224 | tf_op jit(solution)/shard_map/ppermute | solution.py:15
  39.9 2.3 %copy-start.1 = (f32[3,8,2,1024]{3,2,1,0:T(2,128)}, f32[3,8,2,1024]{3,2,1,0:T(2,128)S(1)}, u32[]{:S(2)}) copy-start(f32[3,8,2,1024]{3,2,1,0:T(2,128)S(1)} %get-tuple-element.7) | copy-start | bytes 589828
  40.2 4.1 %collective-permute-start.7 = (f32[2,2,1,2,1024]{4,3,2,1,0:T(2,128)S(1)}, f32[2,2,1,2,1024]{4,3,2,1,0:T(2,128)S(1)}, u32[]{:S(2)}, u32[]{:S(2)}) collective-permute-start(f32[2,2,1,2,1024]{4,3,2,1,0:T(2,128)S(1)} %pad_maximum_fusion.4), channel_id=1, source_target_pairs={{0,2},{2,4},{4,6},{6,8},{8,10},{10,12},{12,14},{14,16},{16,18},{18... | collective-permute-start | bytes 98312 | tf_op jit(solution)/shard_map/ppermute | solution.py:15
  42.5 4.2 %collective-permute-start.6 = (f32[2,2,8,1,1024]{4,3,2,1,0:T(1,128)S(1)}, f32[2,2,8,1,1024]{4,3,2,1,0:T(1,128)S(1)}, u32[]{:S(2)}, u32[]{:S(2)}) collective-permute-start(f32[2,2,8,1,1024]{4,3,2,1,0:T(1,128)S(1)} %fusion.19), channel_id=1, source_target_pairs={{0,1},{2,3},{4,5},{6,7},{8,9},{10,11},{12,13},{14,15},{16,17},{18,... | collective-permute-start | bytes 393224 | tf_op jit(solution)/shard_map/ppermute | solution.py:15
  47.7 1.2 %copy-start.5 = (s32[8,2,1024]{2,1,0:T(2,128)S(1)}, s32[8,2,1024]{2,1,0:T(2,128)}, u32[]{:S(2)}) copy-start(s32[8,2,1024]{2,1,0:T(2,128)} %param.11) | copy-start | bytes 196612
where the time goes:
time: 95 us; the launch traced here: 94.5 us
  blocking collectives  43.3 us (46%)
  waiting for transfers between devices  15.6 us (16%)
  starting transfers between devices  15.5 us (16%)
  other arithmetic  9.33 us (10%)
  local copies, waits for them, and re-layouts  5.4 us (6%)
  between operations  3.9 us (4%)
  matrix products  1.4 us (1%)
    psum x1, blocking collectives, body(): gradient = gradient + lax.psum(partial_sum, ('xy', 'gz'))  43.3 us
    ppermute x8, waiting for transfers between devices, shifted(): lax.ppermute(value, axis, [(source, source + steps) for source in range(l...  15.6 us
    ppermute x8, starting transfers between devices, shifted(): lax.ppermute(value, axis, [(source, source + steps) for source in range(l...  15.5 us
    unnamed x15, local copies, waits for them, and re-layouts  2.36 us
    another operation x8, other arithmetic, body(): first = curl_fwd(jnp.stack([electric[-1], e_coef * adjoint_e[-1]], axis=0))  1.96 us
  transfers between devices with their start and end apart: 8, of which 5 were waited for; matrix products, arithmetic and copies ran while one was open for 2% of the time, Pallas kernels for 0%

commit v1 on v0

v1 whole, which is shorter than its diff:
```python
import functools

import jax
import jax.numpy as jnp
import numpy as np
from jax import lax
from jax.experimental import pallas as pl
from jax.experimental.pallas import tpu as pltpu
from jax.sharding import PartitionSpec as P

NI = 8
COURANT = 0.5
MESH = pl.DeviceIdType.MESH
SCALES = (-COURANT, 1.0)


def kernel(
    dims, e_hbm, h_hbm, g_hbm, k_hbm, mat_hbm, own_hbm, perm,
    go_hbm, ko_hbm, grad_ref,
    field, inner, partial, curl_in, outer, mat, own, coef, weight,
    send_xf, send_xl, send_d5, send_d6,
    got_xf, got_zf, got_xl, got_zl, got_d5, got_d6,
    mine, gathered,
    load_sem, send_sem, recv_sem, sum_send, sum_recv, out_sem,
):
    n_x, n_z, nx, nz, ny, kinds, norm = dims
    total = n_x * n_z
    i = lax.axis_index("xy")
    k = lax.axis_index("gz")
    me = i * n_z + k

    def load(src, dst, slot):
        copies = []
        for z in range(nz):
            src_z = src.at[:, :, z, :] if len(src.shape) == 4 else src.at[:, z, :]
            dst_z = dst.at[:, z] if len(src.shape) == 4 else dst.at[z]
            copies.append(pltpu.make_async_copy(src_z, dst_z, load_sem.at[slot, z]))
        return copies

    loads = [
        load(e_hbm, field.at[0], 0),
        load(h_hbm, inner.at[0], 1),
        load(mat_hbm, mat, 2),
        load(g_hbm, outer, 3),
        load(k_hbm, inner.at[1], 4),
        load(own_hbm, own, 5),
    ]
    for group in loads:
        for copy in group:
            copy.start()

    barrier = pltpu.get_barrier_semaphore()

    def greet(step, carry):
        other = lax.rem(me + step, total)
        pl.semaphore_signal(
            barrier, inc=1, device_id=(other // n_z, lax.rem(other, n_z)), device_id_type=MESH
        )
        return carry

    lax.fori_loop(1, total, greet, 0)

    rows = lax.broadcasted_iota(jnp.int32, (nx, ny), 0)
    lanes = lax.broadcasted_iota(jnp.int32, (nx, ny), 1)
    first_row, last_row = rows == 0, rows == nx - 1
    first_lane, last_lane = lanes == 0, lanes == ny - 1

    def dy(v):
        return jnp.where(last_lane, 0.0, pltpu.roll(v, ny - 1, 1)) - v

    def dx(v):
        return jnp.where(last_row, 0.0, pltpu.roll(v, nx - 1, 0)) - v

    def by(v):
        return v - jnp.where(first_lane, 0.0, pltpu.roll(v, 1, 1))

    def bx(v, row):
        return v - jnp.where(first_row, row, pltpu.roll(v, 1, 0))

    def local_part(q, mag):
        scale = SCALES[q % 2]
        f = field.at[q]
        for z in range(nz):
            fx, fy, fz = f[0, z], f[1, z], f[2, z]
            if z < nz - 1:
                up_x, up_y = f[0, z + 1] - fx, f[1, z + 1] - fy
            else:
                up_x, up_y = -fx, -fy
            lx = mag[0, z] + scale * (dy(fz) - up_y)
            ly = mag[1, z] + scale * (up_x - dx(fz))
            lz = mag[2, z] + scale * (dx(fy) - dy(fx))
            partial[q, 0, z], partial[q, 1, z], partial[q, 2, z] = lx, ly, lz
            send_xf[q, z : z + 1] = fy[0:1]
            send_xf[q, nz + z : nz + z + 1] = fz[0:1]
            send_xl[q, z : z + 1] = ly[nx - 1 : nx]
            send_xl[q, nz + z : nz + z + 1] = lz[nx - 1 : nx]
            if z == 0:
                send_d5[q] = fx[nx - 1 : nx]
            if z == nz - 1:
                send_d6[q] = fz[0:1]

    def messages(q):
        below_x, above_x = i > 0, i < n_x - 1
        below_z, above_z = k > 0, k < n_z - 1
        table = (
            (field.at[q, 0:2, 0], got_zf.at[q], (i, k - 1), below_z, above_z),
            (partial.at[q, 0:2, nz - 1], got_zl.at[q], (i, k + 1), above_z, below_z),
            (send_xf.at[q], got_xf.at[q], (i - 1, k), below_x, above_x),
            (send_xl.at[q], got_xl.at[q], (i + 1, k), above_x, below_x),
            (send_d5.at[q], got_d5.at[q], (i + 1, k - 1), above_x & below_z, below_x & above_z),
            (send_d6.at[q], got_d6.at[q], (i - 1, k + 1), below_x & above_z, above_x & below_z),
        )
        return [
            (
                pltpu.make_async_remote_copy(
                    src_ref=src, dst_ref=dst, send_sem=send_sem.at[q, m],
                    recv_sem=recv_sem.at[q, m], device_id=target, device_id_type=MESH,
                ),
                sends,
                receives,
            )
            for m, (src, dst, target, sends, receives) in enumerate(table)
        ]

    def send(q):
        for copy, sends, _ in messages(q):
            pl.when(sends)(copy.start)

    def receive(q):
        for copy, _, receives in messages(q):
            pl.when(receives)(copy.wait_recv)

    def finish(q, put):
        scale = SCALES[q % 2]
        f, part = field.at[q], partial.at[q]
        not_first_x, not_last_x = i > 0, i < n_x - 1
        not_first_z, not_last_z = k > 0, k < n_z - 1

        def only(cond, v):
            return jnp.where(cond, v, 0.0)

        below_x = only(not_first_z, got_zl[q, 0] - scale * f[1, 0])
        below_y = got_zl[q, 1] + scale * f[0, 0]
        diagonal = only(not_last_x, scale * got_d6[q])
        below_y = only(not_first_z, below_y - jnp.where(last_row, diagonal, 0.0))
        result = []
        for z in range(nz):
            mx, my, mz = part[0, z], part[1, z], part[2, z]
            edge_y = got_xl[q, z : z + 1] - scale * f[2, z, 0:1]
            edge_z = got_xl[q, nz + z : nz + z + 1] + scale * f[1, z, 0:1]
            if z == nz - 1:
                mx = mx - only(not_last_z, scale * got_zf[q, 1])
                my = my + only(not_last_z, scale * got_zf[q, 0])
                edge_y = edge_y + only(not_last_z, scale * got_d5[q])
            edge_y, edge_z = only(not_first_x, edge_y), only(not_first_x, edge_z)
            next_y = only(not_last_x, scale * got_xf[q, z : z + 1])
            next_z = only(not_last_x, scale * got_xf[q, nz + z : nz + z + 1])
            my = my - jnp.where(last_row, next_z, 0.0)
            mz = mz + jnp.where(last_row, next_y, 0.0)
            if put is not None:
                put[0, z], put[1, z], put[2, z] = mx, my, mz
            result.append(
                (
                    by(mz) - (my - below_y),
                    (mx - below_x) - bx(mz, edge_z),
                    bx(my, edge_y) - by(mx),
                )
            )
            below_x, below_y = mx, my
        return result

    for slot in (0, 1):
        for copy in loads[slot]:
            copy.wait()
    local_part(0, inner.at[0])
    for slot in (2, 3, 4):
        for copy in loads[slot]:
            copy.wait()
    for z in range(nz):
        kind = mat[z]
        eps = jnp.full((nx, ny), perm[0], jnp.float32)
        for number in range(1, kinds):
            eps = jnp.where(kind == number, perm[number], eps)
        coef[z] = COURANT / eps
        for c in range(3):
            field[1, c, z] = coef[z] * outer[c, z]
    pl.semaphore_wait(barrier, total - 1)
    send(0)
    local_part(1, inner.at[1])
    send(1)

    receive(0)
    change = finish(0, curl_in.at[0])
    for z in range(nz):
        for c in range(3):
            moved = coef[z] * change[z][c]
            curl_in[2, c, z] = moved
            field[2, c, z] = field[0, c, z] + moved
    local_part(2, curl_in.at[0])
    send(2)

    receive(1)
    change = finish(1, curl_in.at[1])
    for z in range(nz):
        dot = None
        for c in range(3):
            now = outer[c, z] - COURANT * change[z][c]
            inner[1, c, z] = now
            field[3, c, z] = coef[z] * now
            term = now * curl_in[2, c, z]
            dot = term if dot is None else dot + term
        weight[z] = coef[z] * dot
    local_part(3, curl_in.at[1])
    send(3)
    for copy in loads[5]:
        copy.wait()

    receive(2)
    change = finish(2, None)
    sums = [None] * NI
    for z in range(nz):
        dot = None
        for c in range(3):
            term = outer[c, z] * (coef[z] * change[z][c])
            dot = term if dot is None else dot + term
        both = weight[z] + coef[z] * dot
        which = own[z]
        for j in range(NI):
            share = jnp.sum(jnp.where(which == j, both, 0.0), axis=0, keepdims=True)
            sums[j] = share if sums[j] is None else sums[j] + share
    lane = lax.broadcasted_iota(jnp.int32, (1, 128), 1)
    line = jnp.zeros((1, 128), jnp.float32)
    for j in range(NI):
        line = jnp.where(lane == j, jnp.sum(sums[j], axis=1, keepdims=True), line)
    mine[0] = line
    gathered[me] = line

    def share_sum(step, carry):
        other = lax.rem(me + step, total)
        pltpu.make_async_remote_copy(
            src_ref=mine.at[0], dst_ref=gathered.at[me], send_sem=sum_send, recv_sem=sum_recv,
            device_id=(other // n_z, lax.rem(other, n_z)), device_id_type=MESH,
        ).start()
        return carry

    lax.fori_loop(1, total, share_sum, 0)

    receive(3)
    change = finish(3, inner.at[0])
    for z in range(nz):
        for c in range(3):
            outer[c, z] = inner[1, c, z] - COURANT * change[z][c]
    outs = []
    for z in range(nz):
        outs.append(pltpu.make_async_copy(inner.at[0, :, z], ko_hbm.at[:, :, z, :], out_sem.at[0, z]))
        outs.append(pltpu.make_async_copy(outer.at[:, z], go_hbm.at[:, :, z, :], out_sem.at[1, z]))
    for copy in outs:
        copy.start()

    everyone = gathered.at[0 : total - 1]
    pltpu.make_async_copy(everyone, everyone, sum_recv).wait()
    pltpu.make_async_copy(everyone, everyone, sum_send).wait()
    grad_ref[...] = jnp.sum(gathered[...], axis=0)[:, :NI] / norm
    for q in range(4):
        for copy, sends, _ in messages(q):
            pl.when(sends)(copy.wait_send)
    for copy in outs:
        copy.wait()


def solution(mesh):
    n_x, n_z = mesh.shape["xy"], mesh.shape["gz"]

    def body(e_check, h_check, adj_e, adj_h, material, owner, permittivity):
        _, nx, nz, ny = e_check.shape
        cells = nx * n_x * nz * n_z * ny
        norm = np.sqrt(np.float32(cells / NI))
        dims = (n_x, n_z, nx, nz, ny, permittivity.shape[0], norm)
        f32 = jnp.float32
        any_spec = pl.BlockSpec(memory_space=pl.ANY)
        block = (3, nz, nx, ny)
        g, h, grad = pl.pallas_call(
            functools.partial(kernel, dims),
            out_shape=(
                jax.ShapeDtypeStruct(e_check.shape, f32),
                jax.ShapeDtypeStruct(e_check.shape, f32),
                jax.ShapeDtypeStruct((1, NI), f32),
            ),
            in_specs=[any_spec] * 6 + [pl.BlockSpec(memory_space=pltpu.SMEM)],
            out_specs=(any_spec, any_spec, pl.BlockSpec(memory_space=pltpu.VMEM)),
            scratch_shapes=[
                pltpu.VMEM((4,) + block, f32),
                pltpu.VMEM((2,) + block, f32),
                pltpu.VMEM((4,) + block, f32),
                pltpu.VMEM((3,) + block, f32),
                pltpu.VMEM(block, f32),
                pltpu.VMEM((nz, nx, ny), jnp.int32),
                pltpu.VMEM((nz, nx, ny), jnp.int32),
                pltpu.VMEM((nz, nx, ny), f32),
                pltpu.VMEM((nz, nx, ny), f32),
                pltpu.VMEM((4, 2 * nz, ny), f32),
                pltpu.VMEM((4, 2 * nz, ny), f32),
                pltpu.VMEM((4, 1, ny), f32),
                pltpu.VMEM((4, 1, ny), f32),
                pltpu.VMEM((4, 2 * nz, ny), f32),
                pltpu.VMEM((4, 2, nx, ny), f32),
                pltpu.VMEM((4, 2 * nz, ny), f32),
                pltpu.VMEM((4, 2, nx, ny), f32),
                pltpu.VMEM((4, 1, ny), f32),
                pltpu.VMEM((4, 1, ny), f32),
                pltpu.VMEM((1, 1, 128), f32),
                pltpu.VMEM((n_x * n_z, 1, 128), f32),
                pltpu.SemaphoreType.DMA((6, nz)),
                pltpu.SemaphoreType.DMA((4, 6)),
                pltpu.SemaphoreType.DMA((4, 6)),
                pltpu.SemaphoreType.DMA,
                pltpu.SemaphoreType.DMA,
                pltpu.SemaphoreType.DMA((2, nz)),
            ],
            compiler_params=pltpu.CompilerParams(collective_id=0, has_side_effects=True),
            name="yee_adjoint",
        )(e_check, h_check, adj_e, adj_h, material, owner, permittivity)
        return g, h, grad.reshape(NI)

    split = P(None, "xy", "gz", None)
    return jax.shard_map(
        body,
        mesh=mesh,
        in_specs=(split,) * 4 + (P("xy", "gz", None),) * 2 + (P(),),
        out_specs=(split, split, P()),
        check_vma=False,
    )
```

time: 95 us -> 23.9 us (0.25)
  blocking collectives: 43.3 us -> 0 us
  Pallas kernels: 0 us -> 20.2 us
  waiting for transfers between devices: 15.6 us -> 0 us
  starting transfers between devices: 15.5 us -> 0 us
  other arithmetic: 9.33 us -> 0 us
  between operations: 3.9 us -> 0.65 us
  local copies, waits for them, and re-layouts: 5.4 us -> 2.85 us
  matrix products: 1.4 us -> 0 us
    psum x1 -> x0, blocking collectives: 43.3 us -> none  [body(): gradient = gradient + lax.psum(partial_sum, ('xy', 'gz'))]
    pallas_call x0 -> x1, Pallas kernels: none -> 20.2 us  [body(): pl.pallas_call(functools.partial(kernel, dims), out_shape=(jax.ShapeDtype...]
    ppermute x8 -> x0, waiting for transfers between devices: 15.6 us -> none  [shifted(): lax.ppermute(value, axis, [(source, source + steps) for source in range(l...]
    ppermute x8 -> x0, starting transfers between devices: 15.5 us -> none  [shifted(): lax.ppermute(value, axis, [(source, source + steps) for source in range(l...]
    another operation x24 -> x0, other arithmetic: 5.72 us -> none  [the longest x8 1.96 us: body(): first = curl_fwd(jnp.stack([electric[-1], e_coef * adjoint_e[-1]], axis=0))]
    slice x17 -> x0, local copies, waits for them, and re-layouts: 2.52 us -> none  [the longest x1 1.42 us: body(): permittivity[kind_index]]
    dot_general x2 -> x0, matrix products: 1.4 us -> none  [interface_sums(): jnp.dot(weight.reshape(1, -1), onehot, precision=lax.Precision.HIGHEST)[0]]
    reduce_sum x1 -> x0, other arithmetic: 1.18 us -> none  [body(): jnp.sum(adjoint_now * (electric[later_step] - electric[later_step - 1]),...]
  transfers between devices with their start and end apart: 8 -> 0, of which waited for: 5 -> 0; matrix products, arithmetic and copies ran while one was open for 2% -> 0% of each run, Pallas kernels for 0% -> 0%
where the time goes in v1:
time: 23.9 us; the launch traced here: 23.7 us
  Pallas kernels  20.2 us (85%)
  local copies, waits for them, and re-layouts  2.85 us (12%)
  between operations  0.65 us (3%)
    pallas_call x1, Pallas kernels, body(): pl.pallas_call(functools.partial(kernel, dims), out_shape=(jax.ShapeDtype...  20.2 us
    unnamed x7, local copies, waits for them, and re-layouts  2.85 us

profile of v1, /device:TPU:0, one launch (start us, length us, event | category | flops | bytes accessed | tf_op | source)
XLA Modules:
  0.0 23.7 jit_solution(15909315335539873618)
XLA Ops:
  0.6 20.2 %yee_adjoint.1 = (f32[3,8,2,1024]{3,2,1,0:T(2,128)}, f32[3,8,2,1024]{3,2,1,0:T(2,128)}, f32[1,8]{1,0:T(1,128)}) custom-call(f32[3,8,2,1024]{3,2,1,0:T(2,128)} %e_hbm.1, f32[3,8,2,1024]{3,2,1,0:T(2,128)} %h_hbm.1, f32[3,8,2,1024]{3,2,1,0:T(2,128)} %g_hbm.1, f32[3,8,2,1024]{3,2,1,0:T(2,128)} %k_hbm.1, s32[8,2,1024]{2,1,0:T(2,128)} %mat_hbm.1, ...), custom_call_target="tpu_custom_call" | custom-call | tf_op jit(solution)/shard_map/yee_adjoint/pallas_call | solution.py:282
  20.8 0.0 copy-start
  20.9 1.7 %copy.13 = f32[3,8,2,1024]{3,2,1,0:T(2,128)} copy(f32[3,8,2,1024]{3,2,1,0:T(2,128)} %get-tuple-element.12) | data formatting | bytes 393216
  22.5 0.0 copy-done
  22.5 0.0 copy-start.1
  22.5 0.7 %copy.14 = f32[3,8,2,1024]{3,2,1,0:T(2,128)} copy(f32[3,8,2,1024]{3,2,1,0:T(2,128)S(1)} %copy-done) | data formatting | bytes 393216
  23.2 0.0 copy-done.1
  23.2 0.5 %copy.15 = f32[8]{0:T(128)} copy(f32[8]{0:T(128)S(1)} %bitcast.1) | data formatting | bytes 64
Async XLA Ops:
  20.8 1.7 %copy-start = (f32[3,8,2,1024]{3,2,1,0:T(2,128)S(1)}, f32[3,8,2,1024]{3,2,1,0:T(2,128)}, u32[]{:S(2)}) copy-start(f32[3,8,2,1024]{3,2,1,0:T(2,128)} %get-tuple-element.13) | copy-start | bytes 589828
  22.5 0.7 %copy-start.1 = (f32[1,8]{1,0:T(1,128)S(1)}, f32[1,8]{1,0:T(1,128)}, u32[]{:S(2)}) copy-start(f32[1,8]{1,0:T(1,128)} %get-tuple-element.8) | copy-start | bytes 100

commit v2 on v1

--- a/solution.py
+++ b/solution.py
@@ -16,12 +16,12 @@
 
 def kernel(
     dims, e_hbm, h_hbm, g_hbm, k_hbm, mat_hbm, own_hbm, perm,
-    go_hbm, ko_hbm, grad_ref,
+    go_ref, ko_ref, grad_ref,
     field, inner, partial, curl_in, outer, mat, own, coef, weight,
     send_xf, send_xl, send_d5, send_d6,
     got_xf, got_zf, got_xl, got_zl, got_d5, got_d6,
     mine, gathered,
-    load_sem, send_sem, recv_sem, sum_send, sum_recv, out_sem,
+    load_sem, send_sem, recv_sem, sum_send, sum_recv,
 ):
     n_x, n_z, nx, nz, ny, kinds, norm = dims
     total = n_x * n_z
@@ -103,12 +103,12 @@
         below_x, above_x = i > 0, i < n_x - 1
         below_z, above_z = k > 0, k < n_z - 1
         table = (
+            (send_d5.at[q], got_d5.at[q], (i + 1, k - 1), above_x & below_z, below_x & above_z),
+            (send_d6.at[q], got_d6.at[q], (i - 1, k + 1), below_x & above_z, above_x & below_z),
+            (send_xf.at[q], got_xf.at[q], (i - 1, k), below_x, above_x),
+            (send_xl.at[q], got_xl.at[q], (i + 1, k), above_x, below_x),
             (field.at[q, 0:2, 0], got_zf.at[q], (i, k - 1), below_z, above_z),
             (partial.at[q, 0:2, nz - 1], got_zl.at[q], (i, k + 1), above_z, below_z),
-            (send_xf.at[q], got_xf.at[q], (i - 1, k), below_x, above_x),
-            (send_xl.at[q], got_xl.at[q], (i + 1, k), above_x, below_x),
-            (send_d5.at[q], got_d5.at[q], (i + 1, k - 1), above_x & below_z, below_x & above_z),
-            (send_d6.at[q], got_d6.at[q], (i - 1, k + 1), below_x & above_z, above_x & below_z),
         )
         return [
             (
@@ -217,7 +217,7 @@
 
     receive(2)
     change = finish(2, None)
-    sums = [None] * NI
+    sums = [jnp.zeros((nx, 128), jnp.float32)] * NI
     for z in range(nz):
         dot = None
         for c in range(3):
@@ -225,13 +225,15 @@
             dot = term if dot is None else dot + term
         both = weight[z] + coef[z] * dot
         which = own[z]
-        for j in range(NI):
-            share = jnp.sum(jnp.where(which == j, both, 0.0), axis=0, keepdims=True)
-            sums[j] = share if sums[j] is None else sums[j] + share
+        for t in range(0, ny, 128):
+            part, index = both[:, t : t + 128], which[:, t : t + 128]
+            for j in range(NI):
+                sums[j] = sums[j] + jnp.where(index == j, part, 0.0)
     lane = lax.broadcasted_iota(jnp.int32, (1, 128), 1)
     line = jnp.zeros((1, 128), jnp.float32)
     for j in range(NI):
-        line = jnp.where(lane == j, jnp.sum(sums[j], axis=1, keepdims=True), line)
+        column = jnp.sum(sums[j], axis=0, keepdims=True)
+        line = jnp.where(lane == j, jnp.sum(column, axis=1, keepdims=True), line)
     mine[0] = line
     gathered[me] = line
 
@@ -246,17 +248,10 @@
     lax.fori_loop(1, total, share_sum, 0)
 
     receive(3)
-    change = finish(3, inner.at[0])
-    for z in range(nz):
-        for c in range(3):
-            outer[c, z] = inner[1, c, z] - COURANT * change[z][c]
-    outs = []
-    for z in range(nz):
-        outs.append(pltpu.make_async_copy(inner.at[0, :, z], ko_hbm.at[:, :, z, :], out_sem.at[0, z]))
-        outs.append(pltpu.make_async_copy(outer.at[:, z], go_hbm.at[:, :, z, :], out_sem.at[1, z]))
-    for copy in outs:
-        copy.start()
-
+    change = finish(3, ko_ref)
+    for z in range(nz):
+        for c in range(3):
+            go_ref[c, z] = inner[1, c, z] - COURANT * change[z][c]
     everyone = gathered.at[0 : total - 1]
     pltpu.make_async_copy(everyone, everyone, sum_recv).wait()
     pltpu.make_async_copy(everyone, everyone, sum_send).wait()
@@ -264,7 +259,15 @@
     for q in range(4):
         for copy, sends, _ in messages(q):
             pl.when(sends)(copy.wait_send)
-    for copy in outs:
+
+def store(g_ref, h_ref, grad_ref, g_hbm, h_hbm, grad_hbm, sem):
+    copies = [pltpu.make_async_copy(grad_ref, grad_hbm, sem.at[2, 0])]
+    for z in range(g_ref.shape[1]):
+        copies.append(pltpu.make_async_copy(g_ref.at[:, z], g_hbm.at[:, :, z, :], sem.at[0, z]))
+        copies.append(pltpu.make_async_copy(h_ref.at[:, z], h_hbm.at[:, :, z, :], sem.at[1, z]))
+    for copy in copies:
+        copy.start()
+    for copy in copies:
         copy.wait()
 
 
@@ -277,17 +280,16 @@
         norm = np.sqrt(np.float32(cells / NI))
         dims = (n_x, n_z, nx, nz, ny, permittivity.shape[0], norm)
         f32 = jnp.float32
-        any_spec = pl.BlockSpec(memory_space=pl.ANY)
+        hbm_spec = pl.BlockSpec(memory_space=pltpu.HBM)
+        vmem_spec = pl.BlockSpec(memory_space=pltpu.VMEM)
         block = (3, nz, nx, ny)
         g, h, grad = pl.pallas_call(
             functools.partial(kernel, dims),
             out_shape=(
-                jax.ShapeDtypeStruct(e_check.shape, f32),
-                jax.ShapeDtypeStruct(e_check.shape, f32),
-                jax.ShapeDtypeStruct((1, NI), f32),
+                pltpu.VMEM(block, f32), pltpu.VMEM(block, f32), pltpu.VMEM((1, NI), f32),
             ),
-            in_specs=[any_spec] * 6 + [pl.BlockSpec(memory_space=pltpu.SMEM)],
-            out_specs=(any_spec, any_spec, pl.BlockSpec(memory_space=pltpu.VMEM)),
+            in_specs=[hbm_spec] * 6 + [pl.BlockSpec(memory_space=pltpu.SMEM)],
+            out_specs=(vmem_spec,) * 3,
             scratch_shapes=[
                 pltpu.VMEM((4,) + block, f32),
                 pltpu.VMEM((2,) + block, f32),
@@ -315,11 +317,25 @@
                 pltpu.SemaphoreType.DMA((4, 6)),
                 pltpu.SemaphoreType.DMA,
                 pltpu.SemaphoreType.DMA,
-                pltpu.SemaphoreType.DMA((2, nz)),
             ],
-            compiler_params=pltpu.CompilerParams(collective_id=0, has_side_effects=True),
+            compiler_params=pltpu.CompilerParams(
+                collective_id=0, has_side_effects=True
+            ),
             name="yee_adjoint",
         )(e_check, h_check, adj_e, adj_h, material, owner, permittivity)
+        g, h, grad = pl.pallas_call(
+            store,
+            out_shape=(
+                jax.ShapeDtypeStruct(e_check.shape, f32),
+                jax.ShapeDtypeStruct(e_check.shape, f32),
+                jax.ShapeDtypeStruct((1, NI), f32),
+            ),
+            in_specs=[vmem_spec] * 3,
+            out_specs=(hbm_spec,) * 3,
+            scratch_shapes=[pltpu.SemaphoreType.DMA((3, nz))],
+            compiler_params=pltpu.CompilerParams(vmem_limit_bytes=2**20),
+            name="store_outputs",
+        )(g, h, grad)
         return g, h, grad.reshape(NI)
 
     split = P(None, "xy", "gz", None)

time: 23.9 us -> 21.2 us (0.89)
  local copies, waits for them, and re-layouts: 2.85 us -> 0 us
    unnamed x7 -> x0, local copies, waits for them, and re-layouts: 2.85 us -> none
    pallas_call x1 -> x2, Pallas kernels: 20.2 us -> 20.4 us  [the longest x1 19.6 us: body(): pl.pallas_call(functools.partial(kernel, dims), out_shape=(pltpu.VMEM(blo...]
where the time goes in v2:
time: 21.2 us; the launch traced here: 21.1 us
  Pallas kernels  20.4 us (96%)
  between operations  0.64 us (3%)
    pallas_call x1, Pallas kernels, body(): pl.pallas_call(functools.partial(kernel, dims), out_shape=(pltpu.VMEM(blo...  19.6 us
    pallas_call x1, Pallas kernels, body(): pl.pallas_call(store, out_shape=(jax.ShapeDtypeStruct(e_check.shape, f32)...  0.8 us

profile of v2, /device:TPU:0, one launch (start us, length us, event | category | flops | bytes accessed | tf_op | source)
XLA Modules:
  0.0 21.1 jit_solution(5343006992675583598)
XLA Ops:
  0.6 19.6 %yee_adjoint.1 = (f32[3,2,8,1024]{3,2,1,0:T(8,128)S(1)}, f32[3,2,8,1024]{3,2,1,0:T(8,128)S(1)}, f32[1,8]{1,0:T(1,128)S(1)}) custom-call(f32[3,8,2,1024]{3,2,1,0:T(2,128)} %e_hbm.1, f32[3,8,2,1024]{3,2,1,0:T(2,128)} %h_hbm.1, f32[3,8,2,1024]{3,2,1,0:T(2,128)} %g_hbm.1, f32[3,8,2,1024]{3,2,1,0:T(2,128)} %k_hbm.1, s32[8,2,1024]{2,1,0:T(2,128)} %mat_hbm.1, ...), custom_call_target="tpu_custom_call" | custom-call | tf_op jit(solution)/shard_map/yee_adjoint/pallas_call | solution.py:286
  20.3 0.8 %store_outputs.1 = (f32[3,8,2,1024]{3,2,1,0:T(2,128)}, f32[3,8,2,1024]{3,2,1,0:T(2,128)}, f32[1,8]{1,0:T(1,128)}) custom-call(f32[3,2,8,1024]{3,2,1,0:T(8,128)S(1)} %get-tuple-element.9.g_ref, f32[3,2,8,1024]{3,2,1,0:T(8,128)S(1)} %get-tuple-element.10.h_ref, f32[1,8]{1,0:T(1,128)S(1)} %get-tuple-element.11.grad_ref), custom_call_target="tpu_custom_call" | custom-call | tf_op jit(solution)/shard_map/store_outputs/pallas_call | solution.py:326
